TPU v7x, 32 devices: a whole 2x2x4 slice. The times are simulated.
32 devices in a mesh: seq: 8 (over z, x), head: 4 (over y, core).
Axes of the slice: x: 2, y: 2, z: 4, core: 2. Of those that a mesh axis runs over, the one named last changes fastest.
Arguments:
- tokens: bfloat16 [2048, 3584], P('seq'), may hold values from -16 to 16
- length: int32 [1], replicated, may hold values from 512 to 2048
- in_gain: float32 [3584], replicated, may hold values from 0.5 to 1.5
- q_weight: bfloat16 [3584, 3584], P(None, 'head'), may hold values from -0.09375 to 0.09375
- q_bias: float32 [3584], P('head'), may hold values from -60 to 60
- k_weight: bfloat16 [3584, 512], P(None, 'head'), may hold values from -0.09375 to 0.09375
- k_bias: float32 [512], P('head'), may hold values from -60 to 60
- v_weight: bfloat16 [3584, 512], P(None, 'head'), may hold values from -0.09375 to 0.09375
- v_bias: float32 [512], P('head'), may hold values from -2 to 2
- o_weight: bfloat16 [3584, 3584], P('head'), may hold values from -0.125 to 0.125
- final_gain: float32 [3584], P('head'), may hold values from 0.5 to 1.5
Outputs:
- hidden: bfloat16 [2048, 3584], P('seq', 'head')
- embedding: float32 [3584], P('head')
All inputs are finite; a program needn't handle non-finite values.
Results may differ from a plain program's by a relative error of at most 0.0075.
The roundings to bfloat16 on the way count: a program that leaves them out, or rounds other values in their place, can miss the bound.
Values may be sent and summed in bfloat16 or wider, within the bound.
A program may use at most 192 MiB of HBM per device.

v0:
```python
import jax
import jax.numpy as jnp
from jax import lax
from jax.sharding import PartitionSpec as P

D = 3584
HEAD_DIM = 128
rope_base = 1000000.0
epsilon = 1e-06


def rms_norm(inputs, gain):
    inputs = inputs.astype(jnp.float32)
    return inputs * lax.rsqrt(jnp.mean(inputs * inputs, axis=-1, keepdims=True) + epsilon) * gain


def rope_tables(positions):
    half_dim = HEAD_DIM // 2
    inverse = rope_base ** (-(jnp.arange(half_dim, dtype=jnp.float32) * 2.0) / HEAD_DIM)
    angles = positions.astype(jnp.float32)[:, None] * inverse[None, :]
    angles = jnp.concatenate([angles, angles], axis=1)
    return (jnp.cos(angles), jnp.sin(angles))


def rotate(inputs, cosine, sine):
    half_dim = HEAD_DIM // 2
    turned = jnp.concatenate([-inputs[..., half_dim:], inputs[..., :half_dim]], axis=-1)
    return inputs * cosine[:, None, :] + turned * sine[:, None, :]


def key_scores(queries, key_block):
    return lax.dot_general(
        queries, key_block, (((1,), (1,)), ((), ())), preferred_element_type=jnp.float32
    )


def body(
    tokens,
    length,
    in_gain,
    q_weight,
    q_bias,
    k_weight,
    k_bias,
    v_weight,
    v_bias,
    o_weight,
    final_gain,
):
    tok_rows = tokens.shape[0]
    head_count = q_weight.shape[1] // HEAD_DIM
    offset = lax.axis_index("seq") * tok_rows
    limit = length[0]
    positions = offset + jnp.arange(tok_rows, dtype=jnp.int32)
    normed = rms_norm(tokens, in_gain).astype(jnp.bfloat16)
    cosine, sine = rope_tables(positions)
    query = jnp.dot(normed, q_weight, preferred_element_type=jnp.float32) + q_bias
    query = rotate(query.reshape(tok_rows, head_count, HEAD_DIM), cosine, sine) * HEAD_DIM ** (-0.5)
    query = query.astype(jnp.bfloat16).reshape(tok_rows * head_count, HEAD_DIM)
    keys = jnp.dot(normed, k_weight, preferred_element_type=jnp.float32) + k_bias
    keys = (
        rotate(keys.reshape(tok_rows, 1, HEAD_DIM), cosine, sine)
        .astype(jnp.bfloat16)
        .reshape(tok_rows, HEAD_DIM)
    )
    values = (jnp.dot(normed, v_weight, preferred_element_type=jnp.float32) + v_bias).astype(
        jnp.bfloat16
    )
    q_rows = query.shape[0]

    def absorb(carry, piece):
        top, total, accum = carry
        k_piece, v_piece = piece
        count = k_piece.shape[0]
        live = jnp.arange(count, dtype=jnp.int32) < limit
        scores = jnp.where(live[None, :], key_scores(query, k_piece), -1e30)
        new_top = jnp.maximum(top, jnp.max(scores, axis=1))
        weights = jnp.where(live[None, :], jnp.exp(scores - new_top[:, None]), 0.0)
        total = jnp.sum(weights, axis=1)
        accum = jnp.dot(weights.astype(jnp.bfloat16), v_piece, preferred_element_type=jnp.float32)
        return (new_top, total, accum)

    initial = (
        jnp.full((q_rows,), -1e30, jnp.float32),
        jnp.zeros((q_rows,), jnp.float32),
        jnp.zeros((q_rows, HEAD_DIM), jnp.float32),
    )
    piece = (
        lax.all_gather(keys, "seq", axis=0, tiled=True),
        lax.all_gather(values, "seq", axis=0, tiled=True),
    )

    def update(state):
        return absorb(state, piece)

    def unchanged(state):
        return state

    top, total, accum = lax.cond(jnp.int32(0) < limit, update, unchanged, initial)
    attended = (
        (accum / total[:, None]).astype(jnp.bfloat16).reshape(tok_rows, head_count * HEAD_DIM)
    )
    mixed = jnp.dot(attended, o_weight, preferred_element_type=jnp.float32)
    width_share = D // lax.axis_size("head")
    column = lax.axis_index("head") * width_share
    shared = lax.psum_scatter(
        mixed.astype(jnp.bfloat16), "head", scatter_dimension=1, tiled=True
    ).astype(jnp.float32)
    hidden_full = (
        lax.dynamic_slice_in_dim(tokens, column, width_share, 1).astype(jnp.float32) + shared
    )
    squares = lax.psum(jnp.sum(hidden_full * hidden_full, axis=1), "head")
    final = hidden_full * lax.rsqrt(squares[:, None] / D + epsilon) * final_gain
    row_live = positions < limit
    local_sum = jnp.sum(jnp.where(row_live[:, None], final, 0.0), axis=0)
    pooled_sum = lax.psum(local_sum, "seq")
    mean = pooled_sum / limit.astype(jnp.float32)
    power = lax.psum(jnp.sum(mean * mean), "head")
    embedding = mean * lax.rsqrt(power / D + epsilon)
    return (hidden_full.astype(jnp.bfloat16), embedding)


def solution(mesh):
    in_specs = (
        P("seq", None),
        P(),
        P(),
        P(None, "head"),
        P("head"),
        P(None, "head"),
        P("head"),
        P(None, "head"),
        P("head"),
        P("head", None),
        P("head"),
    )
    out_specs = (P("seq", "head"), P("head"))
    return jax.shard_map(body, mesh=mesh, in_specs=in_specs, out_specs=out_specs, check_vma=False)
```

profile of v0, /device:TPU:0, one launch (start us, length us, event | category | flops | bytes accessed | tf_op | source)
XLA Modules:
  0.0 211.3 jit_solution(12068621012374544557)
XLA Ops:
  7.2 2.0 fusion.7
  9.3 6.5 %convolution_add_fusion = f32[256,896]{1,0:T(8,128)} fusion(bf16[3584,896]{1,0:T(8,128)(2,1)} %param.16, f32[896]{0:T(1024)} %param.17, bf16[256,3584]{1,0:T(8,128)(2,1)} %param.13, f32[3584]{0:T(1024)} %param.15, f32[256]{0:T(256)S(1)} %add_rsqrt_fusion.1), kind=kOutput, calls=%fused_computation.16 | convolution fusion | flops 1648066560 | bytes 9193984 | tf_op jit(solution)/shard_map/dot_general | solution.py:57
  15.7 2.6 %copy.23 = f32[256,896]{0,1:T(8,128)} copy(f32[256,896]{1,0:T(8,128)} %convolution_add_fusion) | data formatting | bytes 1835008 | tf_op jit(solution)/shard_map/add | solution.py:57
  18.3 2.2 %reshape.119 = f32[1792,128]{1,0:T(8,128)} reshape(f32[256,896]{1,0:T(8,128)} %convolution_add_fusion) | data formatting | bytes 1835008 | tf_op jit(solution)/shard_map/reshape | solution.py:58
  21.2 0.9 convolution_add_fusion.2
  22.2 1.1 fusion.18
  23.5 33.5 %all_gather.6 = bf16[2048,128]{0,1:T(8,128)(2,1)S(1)} all-gather(bf16[256,128]{0,1:T(8,128)(2,1)} %get-tuple-element.38), channel_id=1, replica_groups=mesh['seq'=8,'head'=4] {'seq'}, dimensions={0}, use_global_device_ids=true | all-gather | bytes 589824 | tf_op jit(solution)/shard_map/all_gather | solution.py:89
  57.0 1.9 fusion.10
  58.9 33.4 %all_gather.7 = bf16[2048,128]{1,0:T(8,128)(2,1)} all-gather(bf16[256,128]{1,0:T(8,128)(2,1)S(1)} %fusion.10), channel_id=1, replica_groups=mesh['seq'=8,'head'=4] {'seq'}, dimensions={0}, use_global_device_ids=true | all-gather | bytes 589824 | tf_op jit(solution)/shard_map/all_gather | solution.py:90
  92.3 0.9 slice_negate_fusion
  93.6 1.0 concatenate.28
  94.7 1.0 mul.131
  95.8 1.1 mul.134
  96.8 1.4 copy.25
  98.3 1.0 concatenate.29
  99.3 2.4 %fusion.13 = bf16[1792,128]{1,0:T(8,128)(2,1)S(1)} fusion(f32[1792,128]{1,0:T(8,128)} %mul.134, f32[1792,64]{1,0:T(8,128)} %concatenate.29, f32[1792,64]{1,0:T(8,128)} %concatenate.28, f32[1792,128]{1,0:T(8,128)S(1)} %copy-done.3, f32[1792,128]{1,0:T(8,128)} %mul.131), kind=kLoop, calls=%fused_computation.23 | loop fusion | flops 1376256 | bytes 4128768 | tf_op jit(solution)/shard_map/convert_element_type | solution.py:59
  101.7 22.9 %conditional.1 = (f32[1792]{0:T(1024)S(1)}, f32[1792,128]{1,0:T(8,128)S(1)}) conditional(s32[]{:T(128)} %convert_element_type.49, () %tuple.16, (s32[]{:T(128)}, bf16[1792,128]{1,0:T(8,128)(2,1)S(1)}, bf16[2048,128]{0,1:T(8,128)(2,1)S(1)}, bf16[2048,128]{1,0:T(8,128)(2,1)S(1)}) %tuple.32), branch_computations={%region_1.0_spmd, %region_2.5_spmd} | conditional | flops 1915748608 | bytes 46516244 | solution.py:99
  101.9 0.7 iota_compare_fusion
  102.6 7.3 %select_reduce_fusion = (f32[1792]{0:T(1024)S(1)}, f32[1792,2048]{1,0:T(8,128)}) fusion(pred[2048]{0:T(1024)(128)(4,1)S(1)} %iota_compare_fusion, bf16[1792,128]{1,0:T(8,128)(2,1)S(1)} %get-tuple-element.9, bf16[2048,128]{0,1:T(8,128)(2,1)S(1)} %get-tuple-element.28), kind=kOutput, calls=%fused_computation.1 | convolution fusion | flops 946862336 | bytes 15672320 | tf_op jit(solution)/shard_map/cond/branch_1_fun/dot_general | solution.py:32
  109.9 8.2 %fusion.1 = f32[1792]{0:T(1024)S(1)} fusion(f32[1792,2048]{1,0:T(8,128)} %get-tuple-element.31, f32[1792]{0:T(1024)S(1)} %broadcast_maximum_fusion, pred[2048]{0:T(1024)(128)(4,1)S(1)} %iota_compare_fusion), kind=kLoop, calls=%fused_computation.3 | loop fusion | flops 14678272 | bytes 14696448 | tf_op jit(solution)/shard_map/cond/branch_1_fun/reduce_sum | solution.py:79
  118.0 6.6 %fusion.2 = f32[1792,128]{1,0:T(8,128)S(1)} fusion(bf16[2048,128]{1,0:T(8,128)(2,1)S(1)} %get-tuple-element.11, f32[1792,2048]{1,0:T(8,128)} %get-tuple-element.31, f32[1792]{0:T(1024)S(1)} %broadcast_maximum_fusion, pred[2048]{0:T(1024)(128)(4,1)S(1)} %iota_compare_fusion), kind=kOutput, calls=%fused_computation.4 | convolution fusion | flops 954204160 | bytes 16131072 | tf_op jit(solution)/shard_map/cond/branch_1_fun/dot_general | solution.py:80
  125.0 0.5 reshape.122
  125.4 6.1 %convolution_convert_fusion = bf16[256,3584]{1,0:T(8,128)(2,1)} fusion(bf16[256,896]{1,0:T(8,128)(2,1)S(1)} %reshape.122, bf16[896,3584]{1,0:T(8,128)(2,1)} %param.22), kind=kOutput, calls=%fused_computation.10 | convolution fusion | flops 1645084672 | bytes 8716288 | tf_op jit(solution)/shard_map/dot_general | solution.py:103
  131.6 4.0 %copy.29 = bf16[256,3584]{0,1:T(8,128)(2,1)} copy(bf16[256,3584]{1,0:T(8,128)(2,1)} %convolution_convert_fusion) | data formatting | bytes 3670016
  135.6 30.9 %reduce-scatter.4.cloned.1.call-done = bf16[896,256]{1,0:T(8,128)(2,1)} async-done(((bf16[3584,256]{1,0:T(8,128)(2,1)}), bf16[896,256]{1,0:T(8,128)(2,1)}) %reduce-scatter.4.cloned.1.call-update) | async-done | bytes 458768
  166.5 1.3 copy.30
  168.0 5.8 %psum.21 = f32[256]{0:T(256)S(1)} all-reduce(f32[256]{0:T(256)S(1)} %multiply_reduce_fusion), channel_id=1, replica_groups=mesh['seq'=8,'head'=4] {'head'}, use_global_device_ids=true, to_apply=%region_7.8 | all-reduce | flops 256 | bytes 2048 | tf_op jit(solution)/shard_map/psum | solution.py:112
  173.8 1.0 select_reduce_fusion.1
  174.8 21.5 %psum.22 = f32[896]{0:T(1024)S(1)} all-reduce(f32[896]{0:T(1024)S(1)} %get-tuple-element.32), channel_id=1, replica_groups=mesh['seq'=8,'head'=4] {'seq'}, use_global_device_ids=true, to_apply=%region_9.10 | all-reduce | flops 896 | bytes 7168 | tf_op jit(solution)/shard_map/psum | solution.py:116
  196.3 0.6 multiply_reduce_fusion.1
  196.9 6.3 %psum.23 = f32[]{:T(128)} all-reduce(f32[]{:T(128)} %multiply_reduce_fusion.1), channel_id=1, replica_groups=mesh['seq'=8,'head'=4] {'head'}, use_global_device_ids=true, to_apply=%region_11.12 | all-reduce | flops 1 | bytes 8 | tf_op jit(solution)/shard_map/psum | solution.py:118
  203.9 0.6 broadcast_multiply_fusion.1
  (37 shorter events, 1.5 us)
Async XLA Ops:
  7.2 14.0 %copy-start = (bf16[3584,128]{1,0:T(8,128)(2,1)S(1)}, bf16[3584,128]{1,0:T(8,128)(2,1)}, u32[]{:S(2)}) copy-start(bf16[3584,128]{1,0:T(8,128)(2,1)} %param.18) | copy-start | bytes 2752516
  7.2 159.3 %reduce-scatter.4.cloned.1.call-start = ((), (), s32[]{:S(2)}) async-start(), calls=%async_computation.1 | async-start | bytes 2293760
  15.7 5.4 %copy-start.1 = (bf16[256,3584]{1,0:T(8,128)(2,1)S(1)}, bf16[256,3584]{1,0:T(8,128)(2,1)}, u32[]{:S(2)}) copy-start(bf16[256,3584]{1,0:T(8,128)(2,1)} %param.13) | copy-start | bytes 5505028
  15.7 5.5 %copy-start.7 = (f32[3584]{0:T(1024)S(1)}, f32[3584]{0:T(1024)}, u32[]{:S(2)}) copy-start(f32[3584]{0:T(1024)} %param.15) | copy-start | bytes 43012
  15.7 5.5 %copy-start.8 = (f32[128]{0:T(128)S(1)}, f32[128]{0:T(128)}, u32[]{:S(2)}) copy-start(f32[128]{0:T(128)} %param.19) | copy-start | bytes 1540
  18.3 38.7 %copy-start.9 = (f32[128]{0:T(128)S(1)}, f32[128]{0:T(128)}, u32[]{:S(2)}) copy-start(f32[128]{0:T(128)} %param.21) | copy-start | bytes 1540
  23.5 68.8 %copy-start.4 = (f32[256,896]{0,1:T(8,128)S(1)}, f32[256,896]{0,1:T(8,128)}, u32[]{:S(2)}) copy-start(f32[256,896]{0,1:T(8,128)} %copy.23) | copy-start | bytes 2752516
  95.7 3.6 %copy-start.3 = (f32[1792,128]{1,0:T(8,128)S(1)}, f32[1792,128]{1,0:T(8,128)}, u32[]{:S(2)}) copy-start(f32[1792,128]{1,0:T(8,128)} %reshape.119) | copy-start | bytes 2752516
  99.3 2.4 %copy-start.5 = (bf16[2048,128]{1,0:T(8,128)(2,1)S(1)}, bf16[2048,128]{1,0:T(8,128)(2,1)}, u32[]{:S(2)}) copy-start(bf16[2048,128]{1,0:T(8,128)(2,1)} %all_gather.7) | copy-start | bytes 1572868
  131.6 36.2 %copy-start.2 = (bf16[256,3584]{1,0:T(8,128)(2,1)S(1)}, bf16[256,3584]{1,0:T(8,128)(2,1)}, u32[]{:S(2)}) copy-start(bf16[256,3584]{1,0:T(8,128)(2,1)} %param.13) | copy-start | bytes 5505028
  131.6 42.2 %copy-start.6 = (f32[896]{0:T(1024)S(1)}, f32[896]{0:T(1024)}, u32[]{:S(2)}) copy-start(f32[896]{0:T(1024)} %param.23) | copy-start | bytes 10756
Sparse Core Ops, SparseCore 0:
  135.7 30.7 reduce-scatter.3
where the time goes:
time: 212 us; the launch traced here: 211 us
  blocking collectives  100 us (47%)
  waiting for transfers between devices  30.9 us (15%)
  matrix products  29.3 us (14%)
  other arithmetic  18.1 us (9%)
  local copies, waits for them, and re-layouts  16.8 us (8%)
  between operations  15.6 us (7%)
    all_gather x1, blocking collectives, body(): lax.all_gather(keys, 'seq', axis=0, tiled=True)  33.5 us
    all_gather x1, blocking collectives, body(): lax.all_gather(values, 'seq', axis=0, tiled=True)  33.4 us
    unnamed x2, waiting for transfers between devices  30.9 us
    psum x1, blocking collectives, body(): pooled_sum = lax.psum(local_sum, 'seq')  21.5 us
    reduce_sum x1, other arithmetic, absorb(): total = jnp.sum(weights, axis=1)  8.15 us
    dot_general x1, matrix products, key_scores(): lax.dot_general(queries, key_block, (((1,), (1,)), ((), ())), preferred_e...  7.28 us
    dot_general x1, matrix products, absorb(): jnp.dot(weights.astype(jnp.bfloat16), v_piece, preferred_element_type=jnp...  6.61 us
    dot_general x1, matrix products, body(): jnp.dot(normed, q_weight, preferred_element_type=jnp.float32) + q_bias  6.46 us
  transfers between devices with their start and end apart: 1, of which 1 were waited for; matrix products, arithmetic and copies ran while one was open for 0% of the time, Pallas kernels for 0%

commit v1 on v0

--- a/solution.py
+++ b/solution.py
@@ -113,7 +113,13 @@
     final = hidden_full * lax.rsqrt(squares[:, None] / D + epsilon) * final_gain
     row_live = positions < limit
     local_sum = jnp.sum(jnp.where(row_live[:, None], final, 0.0), axis=0)
-    pooled_sum = lax.psum(local_sum, "seq")
+    count_2 = lax.axis_size("seq")
+    pooled_sum, stride = (local_sum, 1)
+    while stride < count_2:
+        pooled_sum = pooled_sum + lax.ppermute(
+            pooled_sum, "seq", [(i, i ^ stride) for i in range(count_2)]
+        )
+        stride = 2 * stride
     mean = pooled_sum / limit.astype(jnp.float32)
     power = lax.psum(jnp.sum(mean * mean), "head")
     embedding = mean * lax.rsqrt(power / D + epsilon)

time: 212 us -> 202 us (0.953)
  blocking collectives: 100 us -> 78.9 us
  starting transfers between devices: 0.04 us -> 5.96 us
  waiting for transfers between devices: 30.9 us -> 36.7 us
    psum x1 -> x0, blocking collectives: 21.5 us -> none  [body(): pooled_sum = lax.psum(local_sum, 'seq')]
    ppermute x0 -> x3, starting transfers between devices: none -> 5.93 us  [body(): lax.ppermute(pooled_sum, 'seq', [(i, i ^ stride) for i in range(count_2)])]
    ppermute x0 -> x3, waiting for transfers between devices: none -> 5.79 us  [body(): lax.ppermute(pooled_sum, 'seq', [(i, i ^ stride) for i in range(count_2)])]
  transfers between devices with their start and end apart: 1 -> 4, of which waited for: 1 -> 4; matrix products, arithmetic and copies ran while one was open for 0% -> 0% of each run, Pallas kernels for 0% -> 0%
where the time goes in v1:
time: 202 us
  blocking collectives  78.9 us (39%)
  waiting for transfers between devices  36.7 us (18%)
  matrix products  29.3 us (15%)
  other arithmetic  18.1 us (9%)
  local copies, waits for them, and re-layouts  16.8 us (8%)
  between operations  15.6 us (8%)
  starting transfers between devices  5.96 us (3%)
    all_gather x1, blocking collectives, body(): lax.all_gather(keys, 'seq', axis=0, tiled=True)  33.5 us
    all_gather x1, blocking collectives, body(): lax.all_gather(values, 'seq', axis=0, tiled=True)  33.4 us
    unnamed x2, waiting for transfers between devices  30.9 us
    reduce_sum x1, other arithmetic, absorb(): total = jnp.sum(weights, axis=1)  8.15 us
    dot_general x1, matrix products, key_scores(): lax.dot_general(queries, key_block, (((1,), (1,)), ((), ())), preferred_e...  7.28 us
    dot_general x1, matrix products, absorb(): jnp.dot(weights.astype(jnp.bfloat16), v_piece, preferred_element_type=jnp...  6.61 us
    dot_general x1, matrix products, body(): jnp.dot(normed, q_weight, preferred_element_type=jnp.float32) + q_bias  6.46 us
    psum x1, blocking collectives, body(): power = lax.psum(jnp.sum(mean * mean), 'head')  6.27 us
  transfers between devices with their start and end apart: 4, of which 4 were waited for; matrix products, arithmetic and copies ran while one was open for 0% of the time, Pallas kernels for 0%

profile of v1, /device:TPU:0, one launch (start us, length us, event | category | flops | bytes accessed | tf_op | source)
XLA Modules:
  0.0 201.5 jit_solution(4795228894830560779)
XLA Ops:
  7.2 2.0 fusion.7
  9.3 6.5 %convolution_add_fusion = f32[256,896]{1,0:T(8,128)} fusion(bf16[3584,896]{1,0:T(8,128)(2,1)} %param.16, f32[896]{0:T(1024)} %param.17, bf16[256,3584]{1,0:T(8,128)(2,1)} %param.13, f32[3584]{0:T(1024)} %param.15, f32[256]{0:T(256)S(1)} %add_rsqrt_fusion.1), kind=kOutput, calls=%fused_computation.16 | convolution fusion | flops 1648066560 | bytes 9193984 | tf_op jit(solution)/shard_map/dot_general | solution.py:57
  15.7 2.6 %copy.23 = f32[256,896]{0,1:T(8,128)} copy(f32[256,896]{1,0:T(8,128)} %convolution_add_fusion) | data formatting | bytes 1835008 | tf_op jit(solution)/shard_map/add | solution.py:57
  18.3 2.2 %reshape.119 = f32[1792,128]{1,0:T(8,128)} reshape(f32[256,896]{1,0:T(8,128)} %convolution_add_fusion) | data formatting | bytes 1835008 | tf_op jit(solution)/shard_map/reshape | solution.py:58
  21.2 0.9 convolution_add_fusion.2
  22.2 1.1 fusion.18
  23.5 33.5 %all_gather.6 = bf16[2048,128]{0,1:T(8,128)(2,1)S(1)} all-gather(bf16[256,128]{0,1:T(8,128)(2,1)} %get-tuple-element.38), channel_id=1, replica_groups=mesh['seq'=8,'head'=4] {'seq'}, dimensions={0}, use_global_device_ids=true | all-gather | bytes 589824 | tf_op jit(solution)/shard_map/all_gather | solution.py:89
  57.0 1.9 fusion.10
  58.9 33.4 %all_gather.7 = bf16[2048,128]{1,0:T(8,128)(2,1)} all-gather(bf16[256,128]{1,0:T(8,128)(2,1)S(1)} %fusion.10), channel_id=1, replica_groups=mesh['seq'=8,'head'=4] {'seq'}, dimensions={0}, use_global_device_ids=true | all-gather | bytes 589824 | tf_op jit(solution)/shard_map/all_gather | solution.py:90
  93.6 1.0 concatenate.28
  94.7 1.0 mul.131
  95.8 1.1 mul.134
  96.8 1.4 copy.25
  98.3 1.0 concatenate.29
  99.3 2.4 %fusion.13 = bf16[1792,128]{1,0:T(8,128)(2,1)S(1)} fusion(f32[1792,128]{1,0:T(8,128)} %mul.134, f32[1792,64]{1,0:T(8,128)} %concatenate.29, f32[1792,64]{1,0:T(8,128)} %concatenate.28, f32[1792,128]{1,0:T(8,128)S(1)} %copy-done.3, f32[1792,128]{1,0:T(8,128)} %mul.131), kind=kLoop, calls=%fused_computation.23 | loop fusion | flops 1376256 | bytes 4128768 | tf_op jit(solution)/shard_map/convert_element_type | solution.py:59
  101.7 22.9 %conditional.1 = (f32[1792]{0:T(1024)S(1)}, f32[1792,128]{1,0:T(8,128)S(1)}) conditional(s32[]{:T(128)} %convert_element_type.49, () %tuple.16, (s32[]{:T(128)}, bf16[1792,128]{1,0:T(8,128)(2,1)S(1)}, bf16[2048,128]{0,1:T(8,128)(2,1)S(1)}, bf16[2048,128]{1,0:T(8,128)(2,1)S(1)}) %tuple.32), branch_computations={%region_1.0_spmd, %region_2.5_spmd} | conditional | flops 1915748608 | bytes 46516244 | solution.py:99
  102.6 7.3 %select_reduce_fusion = (f32[1792]{0:T(1024)S(1)}, f32[1792,2048]{1,0:T(8,128)}) fusion(pred[2048]{0:T(1024)(128)(4,1)S(1)} %iota_compare_fusion, bf16[1792,128]{1,0:T(8,128)(2,1)S(1)} %get-tuple-element.9, bf16[2048,128]{0,1:T(8,128)(2,1)S(1)} %get-tuple-element.28), kind=kOutput, calls=%fused_computation.1 | convolution fusion | flops 946862336 | bytes 15672320 | tf_op jit(solution)/shard_map/cond/branch_1_fun/dot_general | solution.py:32
  109.9 8.2 %fusion.1 = f32[1792]{0:T(1024)S(1)} fusion(f32[1792,2048]{1,0:T(8,128)} %get-tuple-element.31, f32[1792]{0:T(1024)S(1)} %broadcast_maximum_fusion, pred[2048]{0:T(1024)(128)(4,1)S(1)} %iota_compare_fusion), kind=kLoop, calls=%fused_computation.3 | loop fusion | flops 14678272 | bytes 14696448 | tf_op jit(solution)/shard_map/cond/branch_1_fun/reduce_sum | solution.py:79
  118.0 6.6 %fusion.2 = f32[1792,128]{1,0:T(8,128)S(1)} fusion(bf16[2048,128]{1,0:T(8,128)(2,1)S(1)} %get-tuple-element.11, f32[1792,2048]{1,0:T(8,128)} %get-tuple-element.31, f32[1792]{0:T(1024)S(1)} %broadcast_maximum_fusion, pred[2048]{0:T(1024)(128)(4,1)S(1)} %iota_compare_fusion), kind=kOutput, calls=%fused_computation.4 | convolution fusion | flops 954204160 | bytes 16131072 | tf_op jit(solution)/shard_map/cond/branch_1_fun/dot_general | solution.py:80
  125.4 6.1 %convolution_convert_fusion = bf16[256,3584]{1,0:T(8,128)(2,1)} fusion(bf16[256,896]{1,0:T(8,128)(2,1)S(1)} %reshape.122, bf16[896,3584]{1,0:T(8,128)(2,1)} %param.22), kind=kOutput, calls=%fused_computation.10 | convolution fusion | flops 1645084672 | bytes 8716288 | tf_op jit(solution)/shard_map/dot_general | solution.py:103
  131.6 4.0 %copy.29 = bf16[256,3584]{0,1:T(8,128)(2,1)} copy(bf16[256,3584]{1,0:T(8,128)(2,1)} %convolution_convert_fusion) | data formatting | bytes 3670016
  135.6 30.9 %reduce-scatter.4.cloned.1.call-done = bf16[896,256]{1,0:T(8,128)(2,1)} async-done(((bf16[3584,256]{1,0:T(8,128)(2,1)}), bf16[896,256]{1,0:T(8,128)(2,1)}) %reduce-scatter.4.cloned.1.call-update) | async-done | bytes 458768
  166.5 1.3 copy.30
  168.0 5.8 %psum.14 = f32[256]{0:T(256)S(1)} all-reduce(f32[256]{0:T(256)S(1)} %multiply_reduce_fusion), channel_id=1, replica_groups=mesh['seq'=8,'head'=4] {'head'}, use_global_device_ids=true, to_apply=%region_7.8 | all-reduce | flops 256 | bytes 2048 | tf_op jit(solution)/shard_map/psum | solution.py:112
  173.8 1.0 select_reduce_fusion.1
  174.8 1.6 collective-permute-start
  176.4 2.0 collective-permute-done
  178.4 1.7 collective-permute-start.1
  180.1 1.9 collective-permute-done.1
  182.0 2.6 %collective-permute-start.2 = (f32[896]{0:T(1024)S(1)}, f32[896]{0:T(1024)S(1)}, u32[]{:S(2)}, u32[]{:S(2)}) collective-permute-start(f32[896]{0:T(1024)S(1)} %add.96), channel_id=1, source_target_pairs={{0,16},{4,20},{8,24},{12,28},{16,0},{20,4},{24,8},{28,12},{1,17},{... | collective-permute-start | bytes 10760 | tf_op jit(solution)/shard_map/ppermute | solution.py:119
  184.6 1.9 collective-permute-done.2
  187.1 6.3 %psum.15 = f32[]{:T(128)} all-reduce(f32[]{:T(128)} %multiply_reduce_fusion.1), channel_id=1, replica_groups=mesh['seq'=8,'head'=4] {'head'}, use_global_device_ids=true, to_apply=%region_10.11 | all-reduce | flops 1 | bytes 8 | tf_op jit(solution)/shard_map/psum | solution.py:124
  (44 shorter events, 4.7 us)
Async XLA Ops:
  7.2 14.0 %copy-start = (bf16[3584,128]{1,0:T(8,128)(2,1)S(1)}, bf16[3584,128]{1,0:T(8,128)(2,1)}, u32[]{:S(2)}) copy-start(bf16[3584,128]{1,0:T(8,128)(2,1)} %param.18) | copy-start | bytes 2752516
  7.2 159.3 %reduce-scatter.4.cloned.1.call-start = ((), (), s32[]{:S(2)}) async-start(), calls=%async_computation.1 | async-start | bytes 2293760
  15.7 5.4 %copy-start.1 = (bf16[256,3584]{1,0:T(8,128)(2,1)S(1)}, bf16[256,3584]{1,0:T(8,128)(2,1)}, u32[]{:S(2)}) copy-start(bf16[256,3584]{1,0:T(8,128)(2,1)} %param.13) | copy-start | bytes 5505028
  15.7 5.5 %copy-start.7 = (f32[3584]{0:T(1024)S(1)}, f32[3584]{0:T(1024)}, u32[]{:S(2)}) copy-start(f32[3584]{0:T(1024)} %param.15) | copy-start | bytes 43012
  15.7 5.5 %copy-start.8 = (f32[128]{0:T(128)S(1)}, f32[128]{0:T(128)}, u32[]{:S(2)}) copy-start(f32[128]{0:T(128)} %param.19) | copy-start | bytes 1540
  18.3 38.7 %copy-start.9 = (f32[128]{0:T(128)S(1)}, f32[128]{0:T(128)}, u32[]{:S(2)}) copy-start(f32[128]{0:T(128)} %param.21) | copy-start | bytes 1540
  23.5 68.8 %copy-start.4 = (f32[256,896]{0,1:T(8,128)S(1)}, f32[256,896]{0,1:T(8,128)}, u32[]{:S(2)}) copy-start(f32[256,896]{0,1:T(8,128)} %copy.23) | copy-start | bytes 2752516
  95.7 3.6 %copy-start.3 = (f32[1792,128]{1,0:T(8,128)S(1)}, f32[1792,128]{1,0:T(8,128)}, u32[]{:S(2)}) copy-start(f32[1792,128]{1,0:T(8,128)} %reshape.119) | copy-start | bytes 2752516
  99.3 2.4 %copy-start.5 = (bf16[2048,128]{1,0:T(8,128)(2,1)S(1)}, bf16[2048,128]{1,0:T(8,128)(2,1)}, u32[]{:S(2)}) copy-start(bf16[2048,128]{1,0:T(8,128)(2,1)} %all_gather.7) | copy-start | bytes 1572868
  131.6 36.2 %copy-start.2 = (bf16[256,3584]{1,0:T(8,128)(2,1)S(1)}, bf16[256,3584]{1,0:T(8,128)(2,1)}, u32[]{:S(2)}) copy-start(bf16[256,3584]{1,0:T(8,128)(2,1)} %param.13) | copy-start | bytes 5505028
  131.6 42.2 %copy-start.6 = (f32[896]{0:T(1024)S(1)}, f32[896]{0:T(1024)}, u32[]{:S(2)}) copy-start(f32[896]{0:T(1024)} %param.23) | copy-start | bytes 10756
  174.8 3.6 %collective-permute-start = (f32[896]{0:T(1024)S(1)}, f32[896]{0:T(1024)S(1)}, u32[]{:S(2)}, u32[]{:S(2)}) collective-permute-start(f32[896]{0:T(1024)S(1)} %get-tuple-element.32), channel_id=1, source_target_pairs={{0,4},{4,0},{8,12},{12,8},{16,20},{20,16},{24,28},{28,24},{1,5},{5... | collective-permute-start | bytes 10760 | tf_op jit(solution)/shard_map/ppermute | solution.py:119
  178.4 3.6 %collective-permute-start.1 = (f32[896]{0:T(1024)S(1)}, f32[896]{0:T(1024)S(1)}, u32[]{:S(2)}, u32[]{:S(2)}) collective-permute-start(f32[896]{0:T(1024)S(1)} %add.95), channel_id=1, source_target_pairs={{0,8},{4,12},{8,0},{12,4},{16,24},{20,28},{24,16},{28,20},{1,9},{5... | collective-permute-start | bytes 10760 | tf_op jit(solution)/shard_map/ppermute | solution.py:119
  182.0 4.5 %collective-permute-start.2 = (f32[896]{0:T(1024)S(1)}, f32[896]{0:T(1024)S(1)}, u32[]{:S(2)}, u32[]{:S(2)}) collective-permute-start(f32[896]{0:T(1024)S(1)} %add.96), channel_id=1, source_target_pairs={{0,16},{4,20},{8,24},{12,28},{16,0},{20,4},{24,8},{28,12},{1,17},{... | collective-permute-start | bytes 10760 | tf_op jit(solution)/shard_map/ppermute | solution.py:119
Sparse Core Ops, SparseCore 0:
  135.7 30.7 reduce-scatter.3
